TPU v7x, 32 devices: a whole 2x2x4 slice. The times are simulated.
32 devices in a mesh: seq: 32 (over z, y, x, core).
Axes of the slice: x: 2, y: 2, z: 4, core: 2. Of those that a mesh axis runs over, the one named last changes fastest.
Arguments:
- inputs: bfloat16 [4096, 4096], P('seq'), may hold values from -6 to 6
- step_sizes: bfloat16 [4096, 4096], P('seq'), may hold values from 0.25 to 2
- cotangent: bfloat16 [4096, 4096], P('seq'), may hold values from -6 to 6
- input_coeffs: float32 [16, 4096], P(None, 'seq'), may hold values from -0.3 to 0.3
- output_coeffs: float32 [16, 4096], P(None, 'seq'), may hold values from -0.3 to 0.3
- decay_rates: float32 [16, 4096], replicated, as said below
Outputs:
- grad_inputs: bfloat16 [4096, 4096], P('seq')
- grad_steps: bfloat16 [4096, 4096], P('seq')
- grad_in_coeffs: float32 [16, 4096], P(None, 'seq')
- grad_out_coeffs: float32 [16, 4096], P(None, 'seq')
- grad_rates: float32 [16, 4096], P(None, 'seq')
Inputs may be any that keep to these rules, and one draw needn't show every extreme that they name: `decay_rates`: every entry lies between 0.1 / 4096 and 0.15.
All inputs are finite; a program needn't handle non-finite values.
Results may differ from a plain program's by a relative error of at most 0.001.
Values sent between devices are 32-bit elements; how exact they have to be, the bound alone decides.
A program may use at most 64 MiB of HBM per device.

v0:
```python
from functools import partial

import jax
import jax.numpy as jnp
from jax import lax
from jax.sharding import PartitionSpec as P

block_len = 32


def from_behind(value, axis, by):
    length = lax.axis_size(axis)
    pairs = [(i, i + by) for i in range(length) if 0 <= i + by < length]
    return lax.ppermute(value, axis, pairs)


def blocked(array):
    return array.reshape(array.shape[0] // block_len, block_len, array.shape[1])


def sweep_forward(initial, inputs, step_sizes, in_rows, decay_rates):

    def per_block(carried, block_data):
        hidden, product = carried
        block_input, block_delta, block_bcoef = block_data
        anchor = hidden
        start_product = product
        for position in range(block_len):
            row_delta = block_delta[position].astype(jnp.float32)
            decay_row = jnp.exp(-row_delta[None, :] * decay_rates)
            drive = (
                block_bcoef[position][:, None]
                * (row_delta * block_input[position].astype(jnp.float32))[None, :]
            )
            hidden = decay_row * hidden + drive
            product = product * decay_row
        return ((hidden, product), (anchor, start_product))

    return lax.scan(
        per_block,
        (initial, jnp.ones_like(initial)),
        (blocked(inputs), blocked(step_sizes), blocked(in_rows)),
    )


def sweep_back(step_sizes, cotangent, out_rows, decay_rates):

    def per_block(later, block_data):
        block_delta, block_ccoef, block_grad = block_data
        for position in reversed(range(block_len)):
            row_delta = block_delta[position].astype(jnp.float32)
            decay_row = jnp.exp(-row_delta[None, :] * decay_rates)
            later = decay_row * (
                block_ccoef[position][:, None] * block_grad[position].astype(jnp.float32)[None, :]
                + later
            )
        return (later, None)

    blank = jnp.zeros(decay_rates.shape, jnp.float32)
    final, _ = lax.scan(
        per_block, blank, (blocked(step_sizes), blocked(out_rows), blocked(cotangent)), reverse=True
    )
    return final


def block_grads(carried, block_data, decay_rates):
    later, grad_rates = carried
    anchor, block_input, block_delta, block_bcoef, block_ccoef, block_grad = block_data
    hidden_list = [anchor]
    for position in range(block_len):
        row_delta = block_delta[position].astype(jnp.float32)
        decay_row = jnp.exp(-row_delta[None, :] * decay_rates)
        drive = (
            block_bcoef[position][:, None]
            * (row_delta * block_input[position].astype(jnp.float32))[None, :]
        )
        hidden_list.append(decay_row * hidden_list[-1] + drive)
    input_rows = [None] * block_len
    step_rows = [None] * block_len
    bcoef_rows = [None] * block_len
    ccoef_rows = [None] * block_len
    for position in reversed(range(block_len)):
        row_delta = block_delta[position].astype(jnp.float32)
        row_input = block_input[position].astype(jnp.float32)
        row_grad = block_grad[position].astype(jnp.float32)
        decay_row = jnp.exp(-row_delta[None, :] * decay_rates)
        grad_state = block_ccoef[position][:, None] * row_grad[None, :] + later
        coeff_sum = jnp.sum(grad_state * block_bcoef[position][:, None], 0)
        weighted = grad_state * decay_row * hidden_list[position]
        input_rows[position] = (row_delta * coeff_sum).astype(jnp.bfloat16)
        step_rows[position] = (row_input * coeff_sum - jnp.sum(weighted * decay_rates, 0)).astype(
            jnp.bfloat16
        )
        bcoef_rows[position] = jnp.sum(grad_state * (row_delta * row_input)[None, :], 1)
        ccoef_rows[position] = jnp.sum(hidden_list[position + 1] * row_grad[None, :], 1)
        grad_rates = grad_rates - weighted * row_delta[None, :]
        later = decay_row * grad_state
    return (
        (later, grad_rates),
        (jnp.stack(input_rows), jnp.stack(step_rows), jnp.stack(bcoef_rows), jnp.stack(ccoef_rows)),
    )


def join_products(first_pair, second_pair):
    return (first_pair[0] * second_pair[0], second_pair[0] * first_pair[1] + second_pair[1])


def forward_hops(pair, joiner):
    devices = lax.axis_size("seq")
    offsets = [1] + [1 << level for level in range(max(devices - 1, 1).bit_length())]
    current = pair
    for order, offset in enumerate(offsets):
        received = from_behind(current, "seq", offset)
        current = received if order == 0 else joiner(received, current)
    return current


def backward_hops(pair, joiner):
    devices = lax.axis_size("seq")
    offsets = [1] + [1 << level for level in range(max(devices - 1, 1).bit_length())]
    current = pair
    for order, offset in enumerate(offsets):
        received = from_behind(current, "seq", -offset)
        current = received if order == 0 else joiner(received, current)
    return current


def shards(inputs, step_sizes, cotangent, input_coeffs, output_coeffs, decay_rates):
    n_state, channels = decay_rates.shape
    in_rows = input_coeffs.T
    out_rows = output_coeffs.T
    blank = jnp.zeros((n_state, channels), jnp.float32)
    back_sum = sweep_back(step_sizes, cotangent, out_rows, decay_rates)
    (end_state, product), (local_anchors, start_products) = sweep_forward(
        blank, inputs, step_sizes, in_rows, decay_rates
    )
    forward_pair = (product, end_state)
    backward_pair = (product, back_sum)
    incoming = forward_hops(forward_pair, join_products)[1]
    outgoing = backward_hops(backward_pair, join_products)[1]
    anchors = local_anchors + start_products * incoming[None]
    block_data = (
        anchors,
        blocked(inputs),
        blocked(step_sizes),
        blocked(in_rows),
        blocked(out_rows),
        blocked(cotangent),
    )
    (_, grad_local), pieces = lax.scan(
        partial(block_grads, decay_rates=decay_rates), (outgoing, blank), block_data, reverse=True
    )
    grad_inputs = pieces[0].reshape(-1, channels)
    grad_steps = pieces[1].reshape(-1, channels)
    grad_in_coeffs = pieces[2].reshape(-1, n_state).T
    grad_out_coeffs = pieces[3].reshape(-1, n_state).T
    grad_rates = lax.psum_scatter(grad_local, "seq", scatter_dimension=1, tiled=True)
    return (grad_inputs, grad_steps, grad_in_coeffs, grad_out_coeffs, grad_rates)


def solution(mesh):
    placed = (P("seq", None), P("seq", None), P("seq", None), P(None, "seq"), P(None, "seq"), P())
    return jax.shard_map(
        shards,
        mesh=mesh,
        in_specs=placed,
        out_specs=(P("seq", None), P("seq", None), P(None, "seq"), P(None, "seq"), P(None, "seq")),
        check_vma=False,
    )
```

profile of v0, /device:TPU:0, one launch (start us, length us, event | category | flops | bytes accessed | tf_op | source)
XLA Modules:
  0.0 641.5 jit_solution(17542522061346965741)
XLA Ops:
  8.0 40.5 %while.57 = (s32[]{:T(128)}, f32[16,4096]{1,0:T(8,128)S(1)}, f32[16,4096]{1,0:T(8,128)S(1)}, f32[4,16,4096]{2,1,0:T(8,128)}, f32[4,16,4096]{2,1,0:T(8,128)S(1)},...) while((s32[]{:T(128)}, f32[16,4096]{1,0:T(8,128)S(1)}, ...), condition=%wide.region_1.2_spmd.clone, body=%wide.region_0.1_spmd.clone.sunk | while | flops 13377570 | bytes 6839321 | solution.py:39
  51.7 32.0 %while.58 = (s32[]{:T(128)}, f32[16,4096]{1,0:T(8,128)}, bf16[4,32,4096]{2,1,0:T(8,128)(2,1)}, f32[16,4096]{1,0:T(8,128)}, f32[4,32,16]{2,1,0:T(8,128)S(1)}, /*i...) while((s32[]{:T(128)}, f32[16,4096]{1,0:T(8,128)}, ...), condition=%wide.region_3.4_spmd.clone, body=%wide.region_2.3_spmd.clone.sunk | while | flops 8847395 | bytes 6560967 | solution.py:60
  86.2 5.1 collective-permute-start.11
  91.3 4.3 collective-permute-start.17
  103.2 5.3 collective-permute-start.18
  110.8 4.3 collective-permute-done.18
  115.2 5.3 collective-permute-start.19
  126.5 9.5 %collective-permute-start.20 = (f32[16,4096]{1,0:T(8,128)S(1)}, f32[16,4096]{1,0:T(8,128)S(1)}, u32[]{:S(2)}, u32[]{:S(2)}) collective-permute-start(f32[16,4096]{1,0:T(8,128)S(1)} %get-tuple-element.790), channel_id=1, source_target_pairs={{0,8},{1,9},{2,10},{3,11},{4,12},{5,13},{6,14},{7,15},{8,16},{9,17... | collective-permute-start | bytes 786440 | tf_op jit(solution)/shard_map/ppermute | solution.py:14
  143.1 12.6 %collective-permute-start.21 = (f32[16,4096]{1,0:T(8,128)S(1)}, f32[16,4096]{1,0:T(8,128)S(1)}, u32[]{:S(2)}, u32[]{:S(2)}) collective-permute-start(f32[16,4096]{1,0:T(8,128)S(1)} %get-tuple-element.788), channel_id=1, source_target_pairs={{0,16},{1,17},{2,18},{3,19},{4,20},{5,21},{6,22},{7,23},{8,24},{9,... | collective-permute-start | bytes 786440 | tf_op jit(solution)/shard_map/ppermute | solution.py:14
  160.5 5.6 collective-permute-done.15
  167.3 8.5 %collective-permute-done.10 = f32[16,4096]{1,0:T(8,128)S(1)} collective-permute-done((f32[16,4096]{1,0:T(8,128)S(1)}, f32[16,4096]{1,0:T(8,128)S(1)}, u32[]{:S(2)}, u32[]{:S(2)}) %collective-permute-start.10) | collective-permute-done | bytes 262176 | tf_op jit(solution)/shard_map/ppermute | solution.py:14
  179.4 313.6 %while.59 = (s32[]{:T(128)}, f32[16,4096]{1,0:T(8,128)S(1)}, f32[16,4096]{1,0:T(8,128)S(1)}, bf16[4,32,4096]{2,1,0:T(8,128)(2,1)}, bf16[4,32,4096]{2,1,0:T(8,128...) while((s32[]{:T(128)}, f32[16,4096]{1,0:T(8,128)S(1)}, ...), condition=%wide.region_133.134_spmd.clone, body=%wide.region_4.133_spmd.clone.sunk | while | flops 57015328 | bytes 59494032 | solution.py:150
  236.5 5.2 stack.750
  241.7 5.2 stack.751
  252.3 4.0 stack.748
  314.9 5.2 stack.750
  320.1 5.2 stack.751
  393.4 5.2 stack.750
  398.6 5.2 stack.751
  409.1 4.0 stack.748
  471.7 5.2 stack.750
  476.9 5.2 stack.751
  487.5 4.0 stack.748
  495.3 139.4 %reduce-scatter.2.cloned.1.call-done = f32[16,128]{1,0:T(8,128)} async-done(((f32[16,4096]{1,0:T(8,128)}), f32[16,128]{1,0:T(8,128)}) %reduce-scatter.2.cloned.1.call-update) | async-done | bytes 8208 | tf_op jit(solution)/shard_map/reduce_scatter | solution.py:157
  (769 shorter events, 370.4 us)
Async XLA Ops:
  7.2 627.5 %reduce-scatter.2.cloned.1.call-start = ((), (), s32[]{:S(2)}) async-start(), calls=%async_computation.1 | async-start | bytes 270336 | tf_op jit(solution)/shard_map/reduce_scatter | solution.py:157
  8.0 43.7 %copy-start.4 = (bf16[128,4096]{1,0:T(8,128)(2,1)S(1)}, bf16[128,4096]{1,0:T(8,128)(2,1)}, u32[]{:S(2)}) copy-start(bf16[128,4096]{1,0:T(8,128)(2,1)} %param.14) | copy-start | bytes 3145732
  48.4 42.9 %collective-permute-start.16 = (f32[16,4096]{1,0:T(8,128)S(1)}, f32[16,4096]{1,0:T(8,128)}, u32[]{:S(2)}, u32[]{:S(2)}) collective-permute-start(f32[16,4096]{1,0:T(8,128)S(1)} %get-tuple-element.459), channel_id=1, source_target_pairs={{0,1},{1,2},{2,3},{3,4},{4,5},{5,6},{6,7},{7,8},{8,9},{9,10},{10,1... | collective-permute-start | bytes 786440 | tf_op jit(solution)/shard_map/ppermute | solution.py:14
  83.6 12.0 %collective-permute-start.5 = (f32[16,4096]{1,0:T(8,128)}, f32[16,4096]{1,0:T(8,128)}, u32[]{:S(2)}, u32[]{:S(2)}) collective-permute-start(f32[16,4096]{1,0:T(8,128)} %get-tuple-element.456), channel_id=1, source_target_pairs={{1,0},{2,1},{3,2},{4,3},{5,4},{6,5},{7,6},{8,7},{9,8},{10,9},{11,1... | collective-permute-start | bytes 786440 | tf_op jit(solution)/shard_map/ppermute | solution.py:14
  84.9 12.0 %collective-permute-start = (f32[16,4096]{1,0:T(8,128)S(1)}, f32[16,4096]{1,0:T(8,128)S(1)}, u32[]{:S(2)}, u32[]{:S(2)}) collective-permute-start(f32[16,4096]{1,0:T(8,128)S(1)} %get-tuple-element.455), channel_id=1, source_target_pairs={{1,0},{2,1},{3,2},{4,3},{5,4},{6,5},{7,6},{8,7},{9,8},{10,9},{11,1... | collective-permute-start | bytes 786440 | tf_op jit(solution)/shard_map/ppermute | solution.py:14
  86.2 12.1 %collective-permute-start.11 = (f32[16,4096]{1,0:T(8,128)S(1)}, f32[16,4096]{1,0:T(8,128)S(1)}, u32[]{:S(2)}, u32[]{:S(2)}) collective-permute-start(f32[16,4096]{1,0:T(8,128)S(1)} %get-tuple-element.455), channel_id=1, source_target_pairs={{0,1},{1,2},{2,3},{3,4},{4,5},{5,6},{6,7},{7,8},{8,9},{9,10},{10,1... | collective-permute-start | bytes 786440 | tf_op jit(solution)/shard_map/ppermute | solution.py:14
  91.3 10.8 %collective-permute-start.17 = (f32[16,4096]{1,0:T(8,128)}, f32[16,4096]{1,0:T(8,128)}, u32[]{:S(2)}, u32[]{:S(2)}) collective-permute-start(f32[16,4096]{1,0:T(8,128)} %collective-permute-done.16), channel_id=1, source_target_pairs={{0,1},{1,2},{2,3},{3,4},{4,5},{5,6},{6,7},{7,8},{8,9},{9,10},{10,1... | collective-permute-start | bytes 786440 | tf_op jit(solution)/shard_map/ppermute | solution.py:14
  95.6 12.8 %collective-permute-start.6 = (f32[16,4096]{1,0:T(8,128)}, f32[16,4096]{1,0:T(8,128)S(1)}, u32[]{:S(2)}, u32[]{:S(2)}) collective-permute-start(f32[16,4096]{1,0:T(8,128)} %collective-permute-done.5), channel_id=1, source_target_pairs={{1,0},{2,1},{3,2},{4,3},{5,4},{6,5},{7,6},{8,7},{9,8},{10,9},{11,1... | collective-permute-start | bytes 786440 | tf_op jit(solution)/shard_map/ppermute | solution.py:14
  96.9 25.7 %collective-permute-start.1 = (f32[16,4096]{1,0:T(8,128)S(1)}, f32[16,4096]{1,0:T(8,128)S(1)}, u32[]{:S(2)}, u32[]{:S(2)}) collective-permute-start(f32[16,4096]{1,0:T(8,128)S(1)} %collective-permute-done), channel_id=1, source_target_pairs={{1,0},{2,1},{3,2},{4,3},{5,4},{6,5},{7,6},{8,7},{9,8},{10,9},{11,1... | collective-permute-start | bytes 786440 | tf_op jit(solution)/shard_map/ppermute | solution.py:14
  98.3 12.5 %collective-permute-start.12 = (f32[16,4096]{1,0:T(8,128)S(1)}, f32[16,4096]{1,0:T(8,128)S(1)}, u32[]{:S(2)}, u32[]{:S(2)}) collective-permute-start(f32[16,4096]{1,0:T(8,128)S(1)} %collective-permute-done.11), channel_id=1, source_target_pairs={{0,1},{1,2},{2,3},{3,4},{4,5},{5,6},{6,7},{7,8},{8,9},{9,10},{10,1... | collective-permute-start | bytes 786440 | tf_op jit(solution)/shard_map/ppermute | solution.py:14
  103.2 11.9 %collective-permute-start.18 = (f32[16,4096]{1,0:T(8,128)S(1)}, f32[16,4096]{1,0:T(8,128)S(1)}, u32[]{:S(2)}, u32[]{:S(2)}) collective-permute-start(f32[16,4096]{1,0:T(8,128)S(1)} %multiply_add_fusion.68), channel_id=1, source_target_pairs={{0,2},{1,3},{2,4},{3,5},{4,6},{5,7},{6,8},{7,9},{8,10},{9,11},{10,... | collective-permute-start | bytes 786440 | tf_op jit(solution)/shard_map/ppermute | solution.py:14
  109.5 13.2 %collective-permute-start.7 = (f32[16,4096]{1,0:T(8,128)S(1)}, f32[16,4096]{1,0:T(8,128)S(1)}, u32[]{:S(2)}, u32[]{:S(2)}) collective-permute-start(f32[16,4096]{1,0:T(8,128)S(1)} %multiply_add_fusion.73), channel_id=1, source_target_pairs={{2,0},{3,1},{4,2},{5,3},{6,4},{7,5},{8,6},{9,7},{10,8},{11,9},{12,... | collective-permute-start | bytes 786440 | tf_op jit(solution)/shard_map/ppermute | solution.py:14
  115.2 10.1 %collective-permute-start.19 = (f32[16,4096]{1,0:T(8,128)S(1)}, f32[16,4096]{1,0:T(8,128)S(1)}, u32[]{:S(2)}, u32[]{:S(2)}) collective-permute-start(f32[16,4096]{1,0:T(8,128)S(1)} %get-tuple-element.792), channel_id=1, source_target_pairs={{0,4},{1,5},{2,6},{3,7},{4,8},{5,9},{6,10},{7,11},{8,12},{9,13},{1... | collective-permute-start | bytes 786440 | tf_op jit(solution)/shard_map/ppermute | solution.py:14
  120.5 5.9 collective-permute-start.13
  122.7 16.4 %collective-permute-start.8 = (f32[16,4096]{1,0:T(8,128)S(1)}, f32[16,4096]{1,0:T(8,128)S(1)}, u32[]{:S(2)}, u32[]{:S(2)}) collective-permute-start(f32[16,4096]{1,0:T(8,128)S(1)} %get-tuple-element.798), channel_id=1, source_target_pairs={{4,0},{5,1},{6,2},{7,3},{8,4},{9,5},{10,6},{11,7},{12,8},{13,9},{1... | collective-permute-start | bytes 786440 | tf_op jit(solution)/shard_map/ppermute | solution.py:14
  124.0 15.1 %collective-permute-start.2 = (f32[16,4096]{1,0:T(8,128)S(1)}, f32[16,4096]{1,0:T(8,128)S(1)}, u32[]{:S(2)}, u32[]{:S(2)}) collective-permute-start(f32[16,4096]{1,0:T(8,128)S(1)} %get-tuple-element.799), channel_id=1, source_target_pairs={{2,0},{3,1},{4,2},{5,3},{6,4},{7,5},{8,6},{9,7},{10,8},{11,9},{12,... | collective-permute-start | bytes 786440 | tf_op jit(solution)/shard_map/ppermute | solution.py:14
  126.5 15.3 %collective-permute-start.20 = (f32[16,4096]{1,0:T(8,128)S(1)}, f32[16,4096]{1,0:T(8,128)S(1)}, u32[]{:S(2)}, u32[]{:S(2)}) collective-permute-start(f32[16,4096]{1,0:T(8,128)S(1)} %get-tuple-element.790), channel_id=1, source_target_pairs={{0,8},{1,9},{2,10},{3,11},{4,12},{5,13},{6,14},{7,15},{8,16},{9,17... | collective-permute-start | bytes 786440 | tf_op jit(solution)/shard_map/ppermute | solution.py:14
  136.0 7.0 %collective-permute-start.14 = (f32[16,4096]{1,0:T(8,128)S(1)}, f32[16,4096]{1,0:T(8,128)S(1)}, u32[]{:S(2)}, u32[]{:S(2)}) collective-permute-start(f32[16,4096]{1,0:T(8,128)S(1)} %get-tuple-element.791), channel_id=1, source_target_pairs={{0,4},{1,5},{2,6},{3,7},{4,8},{5,9},{6,10},{7,11},{8,12},{9,13},{1... | collective-permute-start | bytes 786440 | tf_op jit(solution)/shard_map/ppermute | solution.py:14
  139.2 18.1 %collective-permute-start.9 = (f32[16,4096]{1,0:T(8,128)S(1)}, f32[16,4096]{1,0:T(8,128)S(1)}, u32[]{:S(2)}, u32[]{:S(2)}) collective-permute-start(f32[16,4096]{1,0:T(8,128)S(1)} %get-tuple-element.796), channel_id=1, source_target_pairs={{8,0},{9,1},{10,2},{11,3},{12,4},{13,5},{14,6},{15,7},{16,8},{17,9... | collective-permute-start | bytes 786440 | tf_op jit(solution)/shard_map/ppermute | solution.py:14
  140.5 16.8 %collective-permute-start.3 = (f32[16,4096]{1,0:T(8,128)S(1)}, f32[16,4096]{1,0:T(8,128)S(1)}, u32[]{:S(2)}, u32[]{:S(2)}) collective-permute-start(f32[16,4096]{1,0:T(8,128)S(1)} %get-tuple-element.797), channel_id=1, source_target_pairs={{4,0},{5,1},{6,2},{7,3},{8,4},{9,5},{10,6},{11,7},{12,8},{13,9},{1... | collective-permute-start | bytes 786440 | tf_op jit(solution)/shard_map/ppermute | solution.py:14
  143.1 17.4 %collective-permute-start.21 = (f32[16,4096]{1,0:T(8,128)S(1)}, f32[16,4096]{1,0:T(8,128)S(1)}, u32[]{:S(2)}, u32[]{:S(2)}) collective-permute-start(f32[16,4096]{1,0:T(8,128)S(1)} %get-tuple-element.788), channel_id=1, source_target_pairs={{0,16},{1,17},{2,18},{3,19},{4,20},{5,21},{6,22},{7,23},{8,24},{9,... | collective-permute-start | bytes 786440 | tf_op jit(solution)/shard_map/ppermute | solution.py:14
  155.7 10.4 %collective-permute-start.15 = (f32[16,4096]{1,0:T(8,128)S(1)}, f32[16,4096]{1,0:T(8,128)S(1)}, u32[]{:S(2)}, u32[]{:S(2)}) collective-permute-start(f32[16,4096]{1,0:T(8,128)S(1)} %get-tuple-element.789), channel_id=1, source_target_pairs={{0,8},{1,9},{2,10},{3,11},{4,12},{5,13},{6,14},{7,15},{8,16},{9,17... | collective-permute-start | bytes 786440 | tf_op jit(solution)/shard_map/ppermute | solution.py:14
  157.4 18.4 %collective-permute-start.10 = (f32[16,4096]{1,0:T(8,128)S(1)}, f32[16,4096]{1,0:T(8,128)S(1)}, u32[]{:S(2)}, u32[]{:S(2)}) collective-permute-start(f32[16,4096]{1,0:T(8,128)S(1)} %get-tuple-element.794), channel_id=1, source_target_pairs={{16,0},{17,1},{18,2},{19,3},{20,4},{21,5},{22,6},{23,7},{24,8},{25... | collective-permute-start | bytes 786440 | tf_op jit(solution)/shard_map/ppermute | solution.py:14
  158.9 17.0 %collective-permute-start.4 = (f32[16,4096]{1,0:T(8,128)S(1)}, f32[16,4096]{1,0:T(8,128)S(1)}, u32[]{:S(2)}, u32[]{:S(2)}) collective-permute-start(f32[16,4096]{1,0:T(8,128)S(1)} %get-tuple-element.795), channel_id=1, source_target_pairs={{8,0},{9,1},{10,2},{11,3},{12,4},{13,5},{14,6},{15,7},{16,8},{17,9... | collective-permute-start | bytes 786440 | tf_op jit(solution)/shard_map/ppermute | solution.py:14
  (116 other events, 611.5 us)
Sparse Core Ops, SparseCore 0:
  493.9 140.7 reduce-scatter.1
where the time goes:
time: 648 us; the launch traced here: 642 us
  other arithmetic  297 us (46%)
  waiting for transfers between devices  161 us (25%)
  local copies, waits for them, and re-layouts  96.2 us (15%)
  starting transfers between devices  70.3 us (11%)
  between operations  14.4 us (2%)
    reduce_scatter x1, waiting for transfers between devices, shards(): lax.psum_scatter(grad_local, 'seq', scatter_dimension=1, tiled=True)  139 us
    convert_element_type x128, other arithmetic, block_grads(): (row_input * coeff_sum - jnp.sum(weighted * decay_rates, 0)).astype(jnp.b...  78 us
    ppermute x22, starting transfers between devices, from_behind(): return lax.ppermute(value, axis, pairs)  70.2 us
    reduce_sum x68, other arithmetic, block_grads(): jnp.sum(grad_state * (row_delta * row_input)[None, :], 1)  58.6 us
    reduce_sum x36, other arithmetic, block_grads(): jnp.sum(hidden_list[position + 1] * row_grad[None, :], 1)  56.8 us
    mul x8, other arithmetic, per_block(): row_delta * block_input[position].astype(jnp.float32)  22.9 us
    ppermute x22, waiting for transfers between devices, from_behind(): return lax.ppermute(value, axis, pairs)  21.2 us
    another operation x4, local copies, waits for them, and re-layouts, block_grads(): jnp.stack(ccoef_rows)  20.9 us
  transfers between devices with their start and end apart: 23, of which 7 were waited for; matrix products, arithmetic and copies ran while one was open for 5% of the time, Pallas kernels for 0%

commit v1 on v0

v1 whole, which is shorter than its diff:
```python
from functools import partial
import math

import jax
import jax.numpy as jnp
from jax import lax
from jax.experimental import pallas as pl
from jax.experimental.pallas import tpu as pltpu
from jax.sharding import PartitionSpec as P

LANES = 128
SUB = 8
TILES = 4
GROUP = 8
LOG2E = math.log2(math.e)
LN2 = math.log(2.0)
F32 = jnp.float32
MESH = pl.DeviceIdType.MESH


def expand(coef_ref, wide, tokens, n_state):
    for t in range(tokens):
        wide[t] = jnp.broadcast_to(coef_ref[:, t : t + 1], (n_state, LANES))


def row(ref, k, t):
    return ref[k, pl.ds(t, SUB, stride=0), :]


def lanes_of(k):
    return slice(k * LANES, (k + 1) * LANES)


def part(h):
    return slice(h * SUB, (h + 1) * SUB)


def summary_kernel(x_ref, d_ref, g_ref, b_ref, c_ref, a_ref, out_ref, bx, cx, dl, uu, gg, st):
    tokens, block = x_ref.shape
    n_state = a_ref.shape[0]
    halves, tiles = n_state // SUB, block // LANES

    @pl.when(pl.program_id(0) == 0)
    def _():
        expand(b_ref, bx, tokens, n_state)
        expand(c_ref, cx, tokens, n_state)

    for k in range(tiles):
        delta = d_ref[:, lanes_of(k)].astype(F32)
        dl[k] = delta
        uu[k] = delta * x_ref[:, lanes_of(k)].astype(F32)
        gg[k] = g_ref[:, lanes_of(k)].astype(F32)
    rates = [[a_ref[part(h), lanes_of(k)] * (-LOG2E) for h in range(halves)] for k in range(tiles)]

    def group(i, carry):
        prod, end, back = [[list(c) for c in v] for v in carry]
        for s in range(GROUP):
            t = i * GROUP + s
            bs = [bx[t, part(h), :] for h in range(halves)]
            cs = [cx[t, part(h), :] for h in range(halves)]
            for k in range(tiles):
                delta, u, g = row(dl, k, t), row(uu, k, t), row(gg, k, t)
                for h in range(halves):
                    decay = jnp.exp2(delta * rates[k][h])
                    end[k][h] = decay * end[k][h] + bs[h] * u
                    prod[k][h] = decay * prod[k][h]
                    back[k][h] = back[k][h] + prod[k][h] * (cs[h] * g)
        return prod, end, back

    ones = [[jnp.ones((SUB, LANES), F32)] * halves for _ in range(tiles)]
    zeros = [[jnp.zeros((SUB, LANES), F32)] * halves for _ in range(tiles)]
    results = lax.fori_loop(0, tokens // GROUP, group, (ones, zeros, zeros))
    for v in range(3):
        for k in range(tiles):
            for h in range(halves):
                st[v * n_state + h * SUB : v * n_state + (h + 1) * SUB, lanes_of(k)] = results[v][k][h]
    width = out_ref.shape[2]
    for j in range(block // width):
        out_ref[j] = st[:, j * width : (j + 1) * width]


def greet_all(me, n):
    barrier = pltpu.get_barrier_semaphore()

    def tell(k, _):
        pl.semaphore_signal(barrier, inc=1, device_id=(lax.rem(me + k, n),), device_id_type=MESH)
        return 0

    lax.fori_loop(1, n, tell, 0)
    pl.semaphore_wait(barrier, n - 1)


def exchange_copy(me, n, k, src, dst, send_sem, recv_sem):
    dest = lax.rem(me + k, n)
    return pltpu.make_async_remote_copy(
        src_ref=src.at[dest],
        dst_ref=dst.at[me],
        send_sem=send_sem.at[k],
        recv_sem=recv_sem.at[me],
        device_id=(dest,),
        device_id_type=MESH,
    )


def arrival(me, n, k, src, dst, send_sem, recv_sem):
    origin = lax.rem(me + n - k, n)
    return pltpu.make_async_remote_copy(
        src_ref=src.at[origin],
        dst_ref=dst.at[origin],
        send_sem=send_sem.at[k],
        recv_sem=recv_sem.at[origin],
        device_id=(origin,),
        device_id_type=MESH,
    )


def loop(n, body):
    def step(k, _):
        body(k)
        return 0

    lax.fori_loop(1, n, step, 0)


def chain_kernel(n, send_ref, out_ref, recv, back, send1, recv1, send2, recv2):
    me = lax.axis_index("seq")
    n_state = send_ref.shape[1] // 3
    width = send_ref.shape[2]
    greet_all(me, n)
    first = (send_ref, recv, send1, recv1)
    second = (back, out_ref, send2, recv2)
    loop(n, lambda k: exchange_copy(me, n, k, *first).start())
    recv[me] = send_ref[me]
    loop(n, lambda k: arrival(me, n, k, *first).wait_recv())

    def ahead(d, value):
        back[d, :n_state, :] = value
        return recv[d, :n_state, :] * value + recv[d, n_state : 2 * n_state, :]

    def behind(i, value):
        d = n - 1 - i
        back[d, n_state:, :] = value
        return recv[d, :n_state, :] * value + recv[d, 2 * n_state :, :]

    blank = jnp.zeros((n_state, width), F32)
    lax.fori_loop(0, n, ahead, blank)
    lax.fori_loop(0, n, behind, blank)
    loop(n, lambda k: exchange_copy(me, n, k, *second).start())
    out_ref[me] = back[me]
    loop(n, lambda k: arrival(me, n, k, *second).wait_recv())
    loop(n, lambda k: exchange_copy(me, n, k, *first).wait_send())
    loop(n, lambda k: exchange_copy(me, n, k, *second).wait_send())


def total_kernel(n, send_ref, out_ref, recv, send1, recv1):
    me = lax.axis_index("seq")
    greet_all(me, n)
    refs = (send_ref, recv, send1, recv1)
    loop(n, lambda k: exchange_copy(me, n, k, *refs).start())
    recv[me] = send_ref[me]
    loop(n, lambda k: arrival(me, n, k, *refs).wait_recv())
    out_ref[...] = lax.fori_loop(
        0, n, lambda d, total: total + recv[d], jnp.zeros(out_ref.shape, F32)
    )
    loop(n, lambda k: exchange_copy(me, n, k, *refs).wait_send())


def lane_sums(acc, out_ref, tokens, n_state):
    lane = lax.broadcasted_iota(jnp.int32, (n_state, tokens), 1)
    total = jnp.zeros((n_state, tokens), F32)
    for t in range(tokens):
        total = jnp.where(lane == t, jnp.sum(acc[t], axis=1, keepdims=True), total)
    out_ref[...] = total


def grads_kernel(
    x_ref, d_ref, g_ref, b_ref, c_ref, a_ref, edge_ref,
    gi_ref, gs_ref, gb_ref, gc_ref, gr_ref,
    bx, cx, dl, xx, uu, gg, st, hs, dec, accb, accc, csp, awp, gi, gs,
):
    tokens, block = x_ref.shape
    n_state = a_ref.shape[0]
    halves, tiles = n_state // SUB, block // LANES
    width = edge_ref.shape[2]

    @pl.when(pl.program_id(0) == 0)
    def _():
        expand(b_ref, bx, tokens, n_state)
        expand(c_ref, cx, tokens, n_state)
        accb[...] = jnp.zeros_like(accb)
        accc[...] = jnp.zeros_like(accc)

    for k in range(tiles):
        delta = d_ref[:, lanes_of(k)].astype(F32)
        x = x_ref[:, lanes_of(k)].astype(F32)
        dl[k] = delta
        xx[k] = x
        uu[k] = delta * x
        gg[k] = g_ref[:, lanes_of(k)].astype(F32)
    for j in range(block // width):
        st[:, j * width : (j + 1) * width] = edge_ref[j]
    rates = [[a_ref[part(h), lanes_of(k)] * (-LOG2E) for h in range(halves)] for k in range(tiles)]

    def slot(k, h):
        return slice((k * halves + h) * SUB, (k * halves + h + 1) * SUB)

    def ahead(i, carry):
        hidden = [list(c) for c in carry]
        for s in range(GROUP):
            t = i * GROUP + s
            bs = [bx[t, part(h), :] for h in range(halves)]
            sums = [None] * halves
            for k in range(tiles):
                delta, u, g = row(dl, k, t), row(uu, k, t), row(gg, k, t)
                for h in range(halves):
                    decay = jnp.exp2(delta * rates[k][h])
                    dec[t, slot(k, h), :] = decay
                    hs[t, slot(k, h), :] = hidden[k][h]
                    hidden[k][h] = decay * hidden[k][h] + bs[h] * u
                    term = g * hidden[k][h]
                    sums[h] = term if sums[h] is None else sums[h] + term
            for h in range(halves):
                accc[t, part(h), :] += sums[h]
        return hidden

    start = [[st[part(h), lanes_of(k)] for h in range(halves)] for k in range(tiles)]
    lax.fori_loop(0, tokens // GROUP, ahead, start)

    def behind(i, carry):
        later, rate = [[list(c) for c in v] for v in carry]
        base = tokens - GROUP - i * GROUP
        for s in reversed(range(GROUP)):
            t = base + s
            bs = [bx[t, part(h), :] for h in range(halves)]
            cs = [cx[t, part(h), :] for h in range(halves)]
            sums = [None] * halves
            for k in range(tiles):
                delta, u, g = row(dl, k, t), row(uu, k, t), row(gg, k, t)
                coeff = weigh = None
                for h in range(halves):
                    state = cs[h] * g + later[k][h]
                    later[k][h] = dec[t, slot(k, h), :] * state
                    weighted = later[k][h] * hs[t, slot(k, h), :]
                    rate[k][h] = rate[k][h] + weighted * delta
                    one, two, three = state * bs[h], weighted * rates[k][h], state * u
                    coeff = one if coeff is None else coeff + one
                    weigh = two if weigh is None else weigh + two
                    sums[h] = three if sums[h] is None else sums[h] + three
                csp[k, part(s), :] = coeff
                awp[k, part(s), :] = weigh
            for h in range(halves):
                accb[t, part(h), :] += sums[h]
        rows = pl.ds(pl.multiple_of(base, GROUP), GROUP)
        for k in range(tiles):
            coeff = csp[k, pl.ds(0, GROUP, stride=SUB), :]
            weigh = awp[k, pl.ds(0, GROUP, stride=SUB), :]
            for s in range(1, SUB):
                coeff = coeff + csp[k, pl.ds(s, GROUP, stride=SUB), :]
                weigh = weigh + awp[k, pl.ds(s, GROUP, stride=SUB), :]
            gi[k, rows, :] = dl[k, rows, :] * coeff
            gs[k, rows, :] = xx[k, rows, :] * coeff + LN2 * weigh
        return later, rate

    last = [[st[n_state + h * SUB : n_state + (h + 1) * SUB, lanes_of(k)] for h in range(halves)] for k in range(tiles)]
    zeros = [[jnp.zeros((SUB, LANES), F32)] * halves for _ in range(tiles)]
    _, rate = lax.fori_loop(0, tokens // GROUP, behind, (last, zeros))
    for k in range(tiles):
        gi_ref[:, lanes_of(k)] = gi[k].astype(gi_ref.dtype)
        gs_ref[:, lanes_of(k)] = gs[k].astype(gs_ref.dtype)
        for h in range(halves):
            st[part(h), lanes_of(k)] = -rate[k][h]
    for j in range(block // width):
        gr_ref[j] = st[:n_state, j * width : (j + 1) * width]

    @pl.when(pl.program_id(0) == pl.num_programs(0) - 1)
    def _():
        lane_sums(accb, gb_ref, tokens, n_state)
        lane_sums(accc, gc_ref, tokens, n_state)


def shards(n, inputs, step_sizes, cotangent, input_coeffs, output_coeffs, decay_rates):
    n_state, channels = decay_rates.shape
    tokens = inputs.shape[0]
    width = channels // n
    block = max(TILES * LANES, width)
    tiles = block // LANES
    owners = block // width
    grid = (channels // block,)
    seq_spec = pl.BlockSpec((tokens, block), lambda i: (0, i))
    coef_spec = pl.BlockSpec((n_state, tokens), lambda i: (0, 0))
    rate_spec = pl.BlockSpec((n_state, block), lambda i: (0, i))
    own_spec = lambda rows: pl.BlockSpec((owners, rows, width), lambda i: (i, 0, 0))
    wide = pltpu.VMEM((tokens, n_state, LANES), F32)
    rows = pltpu.VMEM((tiles, tokens, LANES), F32)
    states = pltpu.VMEM((tokens, tiles * n_state, LANES), F32)
    fold = pltpu.VMEM((tiles, GROUP * SUB, LANES), F32)
    vmem = pl.BlockSpec(memory_space=pltpu.VMEM)
    dma = pltpu.SemaphoreType.DMA((n,))
    operands = (inputs, step_sizes, cotangent, input_coeffs, output_coeffs, decay_rates)
    operand_specs = [seq_spec] * 3 + [coef_spec] * 2 + [rate_spec]

    summary = pl.pallas_call(
        summary_kernel,
        name="summary",
        grid=grid,
        in_specs=operand_specs,
        out_specs=own_spec(3 * n_state),
        out_shape=jax.ShapeDtypeStruct((n, 3 * n_state, width), F32),
        scratch_shapes=[wide, wide, rows, rows, rows, pltpu.VMEM((3 * n_state, block), F32)],
        compiler_params=pltpu.CompilerParams(dimension_semantics=("arbitrary",)),
    )(*operands)

    edges = pl.pallas_call(
        partial(chain_kernel, n),
        name="chain",
        in_specs=[vmem],
        out_specs=vmem,
        out_shape=jax.ShapeDtypeStruct((n, 2 * n_state, width), F32),
        scratch_shapes=[
            pltpu.VMEM((n, 3 * n_state, width), F32),
            pltpu.VMEM((n, 2 * n_state, width), F32),
            dma, dma, dma, dma,
        ],
        compiler_params=pltpu.CompilerParams(collective_id=0, has_side_effects=True),
    )(summary)

    gi, gs, gb, gc, gr = pl.pallas_call(
        grads_kernel,
        name="grads",
        grid=grid,
        in_specs=operand_specs + [own_spec(2 * n_state)],
        out_specs=[seq_spec, seq_spec, coef_spec, coef_spec, own_spec(n_state)],
        out_shape=[
            jax.ShapeDtypeStruct((tokens, channels), jnp.bfloat16),
            jax.ShapeDtypeStruct((tokens, channels), jnp.bfloat16),
            jax.ShapeDtypeStruct((n_state, tokens), F32),
            jax.ShapeDtypeStruct((n_state, tokens), F32),
            jax.ShapeDtypeStruct((n, n_state, width), F32),
        ],
        scratch_shapes=[
            wide, wide, rows, rows, rows, rows,
            pltpu.VMEM((2 * n_state, block), F32),
            states, states, wide, wide, fold, fold, rows, rows,
        ],
        compiler_params=pltpu.CompilerParams(
            dimension_semantics=("arbitrary",), vmem_limit_bytes=48 * 1024 * 1024
        ),
    )(*operands, edges)

    grad_rates = pl.pallas_call(
        partial(total_kernel, n),
        name="total",
        in_specs=[vmem],
        out_specs=vmem,
        out_shape=jax.ShapeDtypeStruct((n_state, width), F32),
        scratch_shapes=[pltpu.VMEM((n, n_state, width), F32), dma, dma],
        compiler_params=pltpu.CompilerParams(collective_id=1, has_side_effects=True),
    )(gr)
    return gi, gs, gb, gc, grad_rates


def solution(mesh):
    placed = (P("seq", None), P("seq", None), P("seq", None), P(None, "seq"), P(None, "seq"), P())
    return jax.shard_map(
        partial(shards, mesh.shape["seq"]),
        mesh=mesh,
        in_specs=placed,
        out_specs=(P("seq", None), P("seq", None), P(None, "seq"), P(None, "seq"), P(None, "seq")),
        check_vma=False,
    )
```

time: 648 us -> 110 us (0.17)
  other arithmetic: 297 us -> 0 us
  waiting for transfers between devices: 161 us -> 0 us
  Pallas kernels: 0 us -> 106 us
  local copies, waits for them, and re-layouts: 96.2 us -> 3.05 us
  starting transfers between devices: 70.3 us -> 0 us
  between operations: 14.4 us -> 0.74 us
    reduce_scatter x1 -> x0, waiting for transfers between devices: 139 us -> none  [shards(): lax.psum_scatter(grad_local, 'seq', scatter_dimension=1, tiled=True)]
    reduce_sum x104 -> x0, other arithmetic: 115 us -> none  [the longest x68 58.6 us: block_grads(): jnp.sum(grad_state * (row_delta * row_input)[None, :], 1)]
    pallas_call x0 -> x4, Pallas kernels: none -> 106 us  [the longest x1 41.4 us: shards(): pl.pallas_call(partial(chain_kernel, n), name='chain', in_specs=[vmem], o...]
    convert_element_type x160 -> x0, other arithmetic: 101 us -> none  [the longest x128 78 us: block_grads(): (row_input * coeff_sum - jnp.sum(weighted * decay_rates, 0)).astype(jnp.b...]
    another operation x20 -> x0, local copies, waits for them, and re-layouts: 76.4 us -> none  [the longest x4 20.9 us: block_grads(): jnp.stack(ccoef_rows)]
    ppermute x22 -> x0, starting transfers between devices: 70.2 us -> none  [from_behind(): return lax.ppermute(value, axis, pairs)]
    mul x16 -> x0, other arithmetic: 36.9 us -> none  [the longest x8 22.9 us: per_block(): row_delta * block_input[position].astype(jnp.float32)]
    ppermute x22 -> x0, waiting for transfers between devices: 21.2 us -> none  [from_behind(): return lax.ppermute(value, axis, pairs)]
  transfers between devices with their start and end apart: 23 -> 0, of which waited for: 7 -> 0; matrix products, arithmetic and copies ran while one was open for 5% -> 0% of each run, Pallas kernels for 0% -> 0%
where the time goes in v1:
time: 110 us; the launch traced here: 109 us
  Pallas kernels  106 us (96%)
  local copies, waits for them, and re-layouts  3.05 us (3%)
    pallas_call x1, Pallas kernels, shards(): pl.pallas_call(partial(chain_kernel, n), name='chain', in_specs=[vmem], o...  41.4 us
    pallas_call x1, Pallas kernels, shards(): pl.pallas_call(grads_kernel, name='grads', grid=grid, in_specs=operand_sp...  33.2 us
    pallas_call x1, Pallas kernels, shards(): pl.pallas_call(summary_kernel, name='summary', grid=grid, in_specs=operan...  16.1 us
    pallas_call x1, Pallas kernels, shards(): pl.pallas_call(partial(total_kernel, n), name='total', in_specs=[vmem], o...  15 us
    unnamed x17, local copies, waits for them, and re-layouts  3.05 us

profile of v1, /device:TPU:0, one launch (start us, length us, event | category | flops | bytes accessed | tf_op | source)
XLA Modules:
  0.0 109.4 jit_solution(2932423719263248794)
XLA Ops:
  0.6 0.0 copy-start.1
  0.6 0.0 copy-start.2
  0.7 0.0 copy-start.6
  0.7 0.0 copy-start.7
  0.7 16.1 %summary.1.send_ref = f32[32,48,128]{2,1,0:T(8,128)} custom-call(bf16[128,4096]{1,0:T(8,128)(2,1)} %x_ref.3, bf16[128,4096]{1,0:T(8,128)(2,1)} %d_ref.3, bf16[128,4096]{1,0:T(8,128)(2,1)} %g_ref.3, f32[16,128]{1,0:T(8,128)} %b_ref.3, f32[16,128]{1,0:T(8,128)} %c_ref.3, f32[16,4096]{1,0:T(8,128)} %a_ref.3), custom_call_target="tpu_custom_call" | custom-call | tf_op jit(solution)/shard_map/summary/pallas_call | solution.py:302
  16.7 0.0 copy-start
  16.7 0.0 copy-start.4
  16.8 41.4 %chain.1.edge_ref = f32[32,32,128]{2,1,0:T(8,128)} custom-call(f32[32,48,128]{2,1,0:T(8,128)} %summary.1.send_ref), custom_call_target="tpu_custom_call" | custom-call | tf_op jit(solution)/shard_map/chain/pallas_call | solution.py:313
  58.1 0.0 copy-done.1
  58.1 0.0 copy-done.2
  58.2 0.0 copy-done.6
  58.2 0.0 copy-done.7
  58.2 0.0 copy-done
  58.2 0.0 copy-done.4
  58.2 0.0 copy-start.3
  58.2 1.0 copy-done.3
  59.2 33.2 %grads.1 = (bf16[128,4096]{1,0:T(8,128)(2,1)}, bf16[128,4096]{1,0:T(8,128)(2,1)}, f32[16,128]{1,0:T(8,128)}, f32[16,128]{1,0:T(8,128)}, f32[32,16,128]{2,1,0:T(8,128)S(1)}) custom-call(bf16[128,4096]{1,0:T(8,128)(2,1)S(1)} %copy-done, bf16[128,4096]{1,0:T(8,128)(2,1)S(1)} %copy-done.1, bf16[128,4096]{1,0:T(8,128)(2,1)S(1)} %copy-done.2, ...), custom_call_target="tpu_custom_call" | custom-call | tf_op jit(solution)/shard_map/grads/pallas_call | solution.py:327
  92.4 0.0 copy-start.5
  92.4 0.7 copy-done.5
  93.1 15.0 %total.1 = f32[16,128]{1,0:T(8,128)} custom-call(f32[32,16,128]{2,1,0:T(8,128)} %copy-done.5), custom_call_target="tpu_custom_call" | custom-call | tf_op jit(solution)/shard_map/total/pallas_call | solution.py:350
  108.1 1.3 %copy.12 = f32[16,128]{1,0:T(8,128)} copy(f32[16,128]{1,0:T(8,128)} %total.1) | data formatting | bytes 16384
Async XLA Ops:
  0.6 57.5 %copy-start.1 = (bf16[128,4096]{1,0:T(8,128)(2,1)S(1)}, bf16[128,4096]{1,0:T(8,128)(2,1)}, u32[]{:S(2)}) copy-start(bf16[128,4096]{1,0:T(8,128)(2,1)} %d_ref.3) | copy-start | bytes 3145732
  0.6 57.5 %copy-start.2 = (bf16[128,4096]{1,0:T(8,128)(2,1)S(1)}, bf16[128,4096]{1,0:T(8,128)(2,1)}, u32[]{:S(2)}) copy-start(bf16[128,4096]{1,0:T(8,128)(2,1)} %g_ref.3) | copy-start | bytes 3145732
  0.7 57.5 %copy-start.6 = (f32[16,128]{1,0:T(8,128)S(1)}, f32[16,128]{1,0:T(8,128)}, u32[]{:S(2)}) copy-start(f32[16,128]{1,0:T(8,128)} %b_ref.3) | copy-start | bytes 24580
  0.7 57.5 %copy-start.7 = (f32[16,128]{1,0:T(8,128)S(1)}, f32[16,128]{1,0:T(8,128)}, u32[]{:S(2)}) copy-start(f32[16,128]{1,0:T(8,128)} %c_ref.3) | copy-start | bytes 24580
  16.7 41.4 %copy-start = (bf16[128,4096]{1,0:T(8,128)(2,1)S(1)}, bf16[128,4096]{1,0:T(8,128)(2,1)}, u32[]{:S(2)}) copy-start(bf16[128,4096]{1,0:T(8,128)(2,1)} %x_ref.3) | copy-start | bytes 3145732
  16.7 41.4 %copy-start.4 = (f32[16,4096]{1,0:T(8,128)S(1)}, f32[16,4096]{1,0:T(8,128)}, u32[]{:S(2)}) copy-start(f32[16,4096]{1,0:T(8,128)} %a_ref.3) | copy-start | bytes 786436
  58.2 1.0 copy-start.3
  92.4 0.7 copy-start.5

commit v2 on v0

v2 whole, which is shorter than its diff:
```python
from functools import partial
import math

import jax
import jax.numpy as jnp
from jax import lax
from jax.experimental import pallas as pl
from jax.experimental.pallas import tpu as pltpu
from jax.sharding import PartitionSpec as P

LANES = 128
SUB = 8
TILES = 4
GROUP = 8
LOG2E = math.log2(math.e)
LN2 = math.log(2.0)
F32 = jnp.float32
MESH = pl.DeviceIdType.MESH


def expand(coef_ref, wide, tokens, n_state):
    for t in range(tokens):
        wide[t] = jnp.broadcast_to(coef_ref[:, t : t + 1], (n_state, LANES))


def row(ref, t, n_state):
    return ref[:, pl.ds(t, n_state, stride=0), :]


def lanes_of(k):
    return slice(k * LANES, (k + 1) * LANES)


def loop(start, stop, body):
    def step(k, _):
        body(k)
        return 0

    lax.fori_loop(start, stop, step, 0)


def lane_sums(acc, out_ref, tokens, n_state):
    lane = lax.broadcasted_iota(jnp.int32, (n_state, tokens), 1)
    total = jnp.zeros((n_state, tokens), F32)
    for t in range(tokens):
        total = jnp.where(lane == t, jnp.sum(acc[t], axis=1, keepdims=True), total)
    out_ref[...] = total


def whole_kernel(
    n, block,
    x_ref, d_ref, g_ref, b_ref, c_ref, a_ref,
    gi_ref, gs_ref, gb_ref, gc_ref, gr_ref,
    bx, cx, dl, xx, uu, gg, rt, st, hs, dec, accb, accc, csp, awp, gi, gs,
    out1, in1, out2, in2, out3, in3, send1, recv1, send2, recv2, send3, recv3,
):
    me = lax.axis_index("seq")
    tokens, channels = x_ref.shape
    n_state = a_ref.shape[0]
    tiles, width = block // LANES, channels // n
    blocks, owners = channels // block, block // width
    home = me // owners
    barrier = pltpu.get_barrier_semaphore()

    def tell(k):
        pl.semaphore_signal(barrier, inc=1, device_id=(lax.rem(me + k, n),), device_id_type=MESH)

    def copy(src, dst, send_sem, recv_sem, dest, slot):
        return pltpu.make_async_remote_copy(
            src_ref=src.at[dest],
            dst_ref=dst.at[slot],
            send_sem=send_sem.at[dest],
            recv_sem=recv_sem.at[slot],
            device_id=(dest,),
            device_id_type=MESH,
        )

    first = (out1, in1, send1, recv1)
    second = (out2, in2, send2, recv2)
    third = (out3, in3, send3, recv3)

    def stage(b):
        for k in range(tiles):
            lanes = pl.ds(pl.multiple_of(b * block + k * LANES, LANES), LANES)
            delta = d_ref[:, lanes].astype(F32)
            x = x_ref[:, lanes].astype(F32)
            dl[k] = delta
            xx[k] = x
            uu[k] = delta * x
            gg[k] = g_ref[:, lanes].astype(F32)
            rt[k] = a_ref[:, lanes] * (-LOG2E)

    loop(1, n, tell)
    expand(b_ref, bx, tokens, n_state)
    expand(c_ref, cx, tokens, n_state)
    accb[...] = jnp.zeros_like(accb)
    accc[...] = jnp.zeros_like(accc)
    state_shape = (tiles, n_state, LANES)

    def summarize(order):
        b = lax.rem(home + 1 + order, blocks)
        stage(b)
        rates = rt[...]

        def group(i, carry):
            prod, end, back = carry
            for s in range(GROUP):
                t = i * GROUP + s
                decay = jnp.exp2(row(dl, t, n_state) * rates)
                end = decay * end + bx[t][None] * row(uu, t, n_state)
                prod = decay * prod
                back = back + prod * (cx[t][None] * row(gg, t, n_state))
            return prod, end, back

        zero = jnp.zeros(state_shape, F32)
        _, end, back = lax.fori_loop(
            0, tokens // GROUP, group, (jnp.ones(state_shape, F32), zero, zero)
        )
        for k in range(tiles):
            st[:n_state, lanes_of(k)] = end[k]
            st[n_state : 2 * n_state, lanes_of(k)] = back[k]
            st[2 * n_state :, lanes_of(k)] = jnp.broadcast_to(
                jnp.sum(dl[k], axis=0, keepdims=True), (SUB, LANES)
            )

        @pl.when(order == 0)
        def _():
            pl.semaphore_wait(barrier, n - 1)

        for j in range(owners):
            dest = b * owners + j
            out1[dest] = st[:, j * width : (j + 1) * width]

            @pl.when(dest != me)
            def _():
                copy(*first, dest, me).start()

    loop(0, blocks, summarize)
    in1[me] = out1[me]

    def arrived(refs):
        def wait(k):
            origin = lax.rem(me + n - k, n)
            copy(*refs, origin, origin).wait_recv()

        loop(1, n, wait)

    arrived(first)
    if width % LANES == 0:
        own = a_ref[:, pl.ds(pl.multiple_of(me * width, LANES), width)] * (-LOG2E)
    else:
        own = jnp.zeros((n_state, width), F32)
        for j in range(n):
            own = jnp.where(me == j, a_ref[:, j * width : (j + 1) * width] * (-LOG2E), own)

    def scan(i, carry):
        ahead, behind = carry
        d, e = i, n - 1 - i
        out2[d, :n_state, :] = ahead
        out2[e, n_state:, :] = behind
        ahead = jnp.exp2(own * in1[d, 2 * n_state : 2 * n_state + 1, :]) * ahead + in1[d, :n_state, :]
        behind = (
            jnp.exp2(own * in1[e, 2 * n_state : 2 * n_state + 1, :]) * behind
            + in1[e, n_state : 2 * n_state, :]
        )
        return ahead, behind

    blank = jnp.zeros((n_state, width), F32)
    lax.fori_loop(0, n, scan, (blank, blank))
    loop(1, n, lambda k: copy(*second, lax.rem(me + n - k, n), me).start())
    in2[me] = out2[me]

    def differentiate(order, _):
        b = lax.rem(home + order, blocks)
        stage(b)
        for j in range(owners):
            origin = b * owners + j

            @pl.when(origin != me)
            def _():
                copy(*second, origin, origin).wait_recv()

            st[: 2 * n_state, j * width : (j + 1) * width] = in2[origin]
        rates = rt[...]

        def ahead(i, hidden):
            for s in range(GROUP):
                t = i * GROUP + s
                decay = jnp.exp2(row(dl, t, n_state) * rates)
                dec[t] = decay
                hs[t] = hidden
                hidden = decay * hidden + bx[t][None] * row(uu, t, n_state)
                accc[t] += jnp.sum(row(gg, t, n_state) * hidden, axis=0)
            return hidden

        start = jnp.stack([st[:n_state, lanes_of(k)] for k in range(tiles)])
        lax.fori_loop(0, tokens // GROUP, ahead, start)

        def behind(i, carry):
            later, rate = carry
            base = tokens - GROUP - i * GROUP
            for s in reversed(range(GROUP)):
                t = base + s
                bs = bx[t][None]
                state = cx[t][None] * row(gg, t, n_state) + later
                later = dec[t] * state
                weighted = later * hs[t]
                rate = rate + weighted * row(dl, t, n_state)
                one, two = state * bs, weighted * rates
                fold = slice(s * SUB, (s + 1) * SUB)
                csp[:, fold, :] = sum(one[:, h : h + SUB] for h in range(0, n_state, SUB))
                awp[:, fold, :] = sum(two[:, h : h + SUB] for h in range(0, n_state, SUB))
                accb[t] += jnp.sum(state * row(uu, t, n_state), axis=0)
            rows = pl.ds(pl.multiple_of(base, GROUP), GROUP)
            coeff = csp[:, pl.ds(0, GROUP, stride=SUB), :]
            weigh = awp[:, pl.ds(0, GROUP, stride=SUB), :]
            for s in range(1, SUB):
                coeff = coeff + csp[:, pl.ds(s, GROUP, stride=SUB), :]
                weigh = weigh + awp[:, pl.ds(s, GROUP, stride=SUB), :]
            gi[:, rows, :] = dl[:, rows, :] * coeff
            gs[:, rows, :] = xx[:, rows, :] * coeff + LN2 * weigh
            return later, rate

        last = jnp.stack([st[n_state : 2 * n_state, lanes_of(k)] for k in range(tiles)])
        _, rate = lax.fori_loop(
            0, tokens // GROUP, behind, (last, jnp.zeros(state_shape, F32))
        )
        for k in range(tiles):
            lanes = pl.ds(pl.multiple_of(b * block + k * LANES, LANES), LANES)
            gi_ref[:, lanes] = gi[k].astype(gi_ref.dtype)
            gs_ref[:, lanes] = gs[k].astype(gs_ref.dtype)
            st[:n_state, lanes_of(k)] = -rate[k]
        for j in range(owners):
            dest = b * owners + j
            out3[dest] = st[:n_state, j * width : (j + 1) * width]

            @pl.when(dest != me)
            def _():
                copy(*third, dest, me).start()

        return 0

    lax.fori_loop(0, blocks, differentiate, 0)
    in3[me] = out3[me]
    lane_sums(accb, gb_ref, tokens, n_state)
    lane_sums(accc, gc_ref, tokens, n_state)
    arrived(third)
    gr_ref[...] = lax.fori_loop(0, n, lambda d, total: total + in3[d], blank)
    for refs in (first, second, third):
        loop(1, n, lambda k: copy(*refs, lax.rem(me + k, n), me).wait_send())


def shards(n, inputs, step_sizes, cotangent, input_coeffs, output_coeffs, decay_rates):
    n_state, channels = decay_rates.shape
    tokens = inputs.shape[0]
    width = channels // n
    block = max(TILES * LANES, width)
    tiles = block // LANES
    wide = pltpu.VMEM((tokens, n_state, LANES), F32)
    rows = pltpu.VMEM((tiles, tokens, LANES), F32)
    states = pltpu.VMEM((tokens, tiles, n_state, LANES), F32)
    fold = pltpu.VMEM((tiles, GROUP * SUB, LANES), F32)
    vmem = pl.BlockSpec(memory_space=pltpu.VMEM)
    dma = pltpu.SemaphoreType.DMA((n,))
    head_rows = 2 * n_state + SUB
    slots = lambda count: [pltpu.VMEM((n, count, width), F32)] * 2
    return pl.pallas_call(
        partial(whole_kernel, n, block),
        name="whole",
        in_specs=[vmem] * 6,
        out_specs=[vmem] * 5,
        out_shape=[
            jax.ShapeDtypeStruct((tokens, channels), jnp.bfloat16),
            jax.ShapeDtypeStruct((tokens, channels), jnp.bfloat16),
            jax.ShapeDtypeStruct((n_state, tokens), F32),
            jax.ShapeDtypeStruct((n_state, tokens), F32),
            jax.ShapeDtypeStruct((n_state, width), F32),
        ],
        scratch_shapes=[
            wide, wide, rows, rows, rows, rows,
            pltpu.VMEM((tiles, n_state, LANES), F32),
            pltpu.VMEM((head_rows, block), F32),
            states, states, wide, wide, fold, fold, rows, rows,
            *slots(head_rows), *slots(2 * n_state), *slots(n_state),
            dma, dma, dma, dma, dma, dma,
        ],
        compiler_params=pltpu.CompilerParams(
            collective_id=0, has_side_effects=True, vmem_limit_bytes=60 * 1024 * 1024
        ),
    )(inputs, step_sizes, cotangent, input_coeffs, output_coeffs, decay_rates)


def solution(mesh):
    placed = (P("seq", None), P("seq", None), P("seq", None), P(None, "seq"), P(None, "seq"), P())
    return jax.shard_map(
        partial(shards, mesh.shape["seq"]),
        mesh=mesh,
        in_specs=placed,
        out_specs=(P("seq", None), P("seq", None), P(None, "seq"), P(None, "seq"), P(None, "seq")),
        check_vma=False,
    )
```

time: 648 us -> 74.6 us (0.12)
  other arithmetic: 297 us -> 0 us
  waiting for transfers between devices: 161 us -> 0 us
  local copies, waits for them, and re-layouts: 96.2 us -> 5.35 us
  starting transfers between devices: 70.3 us -> 0 us
  Pallas kernels: 0 us -> 68.3 us
  between operations: 14.4 us -> 0.65 us
    reduce_scatter x1 -> x0, waiting for transfers between devices: 139 us -> none  [shards(): lax.psum_scatter(grad_local, 'seq', scatter_dimension=1, tiled=True)]
    reduce_sum x104 -> x0, other arithmetic: 115 us -> none  [the longest x68 58.6 us: block_grads(): jnp.sum(grad_state * (row_delta * row_input)[None, :], 1)]
    convert_element_type x160 -> x0, other arithmetic: 101 us -> none  [the longest x128 78 us: block_grads(): (row_input * coeff_sum - jnp.sum(weighted * decay_rates, 0)).astype(jnp.b...]
    another operation x20 -> x0, local copies, waits for them, and re-layouts: 76.4 us -> none  [the longest x4 20.9 us: block_grads(): jnp.stack(ccoef_rows)]
    ppermute x22 -> x0, starting transfers between devices: 70.2 us -> none  [from_behind(): return lax.ppermute(value, axis, pairs)]
    pallas_call x0 -> x1, Pallas kernels: none -> 68.3 us  [shards(): pl.pallas_call(partial(whole_kernel, n, block), name='whole', in_specs=[v...]
    mul x16 -> x0, other arithmetic: 36.9 us -> none  [the longest x8 22.9 us: per_block(): row_delta * block_input[position].astype(jnp.float32)]
    ppermute x22 -> x0, waiting for transfers between devices: 21.2 us -> none  [from_behind(): return lax.ppermute(value, axis, pairs)]
  transfers between devices with their start and end apart: 23 -> 0, of which waited for: 7 -> 0; matrix products, arithmetic and copies ran while one was open for 5% -> 0% of each run, Pallas kernels for 0% -> 0%
where the time goes in v2:
time: 74.6 us; the launch traced here: 74.3 us
  Pallas kernels  68.3 us (92%)
  local copies, waits for them, and re-layouts  5.35 us (7%)
    pallas_call x1, Pallas kernels, shards(): pl.pallas_call(partial(whole_kernel, n, block), name='whole', in_specs=[v...  68.3 us
    unnamed x13, local copies, waits for them, and re-layouts  5.35 us

profile of v2, /device:TPU:0, one launch (start us, length us, event | category | flops | bytes accessed | tf_op | source)
XLA Modules:
  0.0 74.3 jit_solution(2390099215259685587)
XLA Ops:
  0.6 68.3 %whole.1 = (bf16[128,4096]{1,0:T(8,128)(2,1)}, bf16[128,4096]{1,0:T(8,128)(2,1)}, f32[16,128]{1,0:T(8,128)}, f32[16,128]{1,0:T(8,128)}, f32[16,128]{1,0:T(8,128)}) custom-call(bf16[128,4096]{1,0:T(8,128)(2,1)} %x_ref.1, bf16[128,4096]{1,0:T(8,128)(2,1)} %d_ref.1, bf16[128,4096]{1,0:T(8,128)(2,1)} %g_ref.1, f32[16,128]{1,0:T(8,128)} %b_ref.1, ...), custom_call_target="tpu_custom_call" | custom-call | tf_op jit(solution)/shard_map/whole/pallas_call | solution.py:267
  69.0 0.0 copy-start
  69.0 2.4 %copy.16 = bf16[128,4096]{1,0:T(8,128)(2,1)} copy(bf16[128,4096]{1,0:T(8,128)(2,1)} %get-tuple-element.10) | data formatting | bytes 2097152
  71.4 0.0 copy-done
  71.4 0.0 copy-start.3
  71.4 1.0 %copy.17 = bf16[128,4096]{1,0:T(8,128)(2,1)} copy(bf16[128,4096]{1,0:T(8,128)(2,1)S(1)} %copy-done) | data formatting | bytes 2097152
  72.3 0.0 copy-done.3
  72.3 0.0 copy-start.2
  72.3 0.6 copy.18
  72.9 0.1 copy-done.2
  73.0 0.0 copy-start.1
  73.0 0.6 copy.19
  73.6 0.1 copy-done.1
  73.7 0.6 copy.20
Async XLA Ops:
  69.0 2.4 %copy-start = (bf16[128,4096]{1,0:T(8,128)(2,1)S(1)}, bf16[128,4096]{1,0:T(8,128)(2,1)}, u32[]{:S(2)}) copy-start(bf16[128,4096]{1,0:T(8,128)(2,1)} %get-tuple-element.11) | copy-start | bytes 3145732
  71.4 1.0 %copy-start.3 = (f32[16,128]{1,0:T(8,128)S(1)}, f32[16,128]{1,0:T(8,128)}, u32[]{:S(2)}) copy-start(f32[16,128]{1,0:T(8,128)} %get-tuple-element.12) | copy-start | bytes 24580
  72.3 0.7 copy-start.2
  73.0 0.7 copy-start.1

commit v3 on v2

--- a/solution.py
+++ b/solution.py
@@ -120,7 +120,7 @@
             st[:n_state, lanes_of(k)] = end[k]
             st[n_state : 2 * n_state, lanes_of(k)] = back[k]
             st[2 * n_state :, lanes_of(k)] = jnp.broadcast_to(
-                jnp.sum(dl[k], axis=0, keepdims=True), (SUB, LANES)
+                jnp.sum(dl[k], axis=0, keepdims=True), (1, LANES)
             )
 
         @pl.when(order == 0)
@@ -166,7 +166,7 @@
         return ahead, behind
 
     blank = jnp.zeros((n_state, width), F32)
-    lax.fori_loop(0, n, scan, (blank, blank))
+    lax.fori_loop(0, n, scan, (blank, blank), unroll=4)
     loop(1, n, lambda k: copy(*second, lax.rem(me + n - k, n), me).start())
     in2[me] = out2[me]
 
@@ -262,7 +262,7 @@
     fold = pltpu.VMEM((tiles, GROUP * SUB, LANES), F32)
     vmem = pl.BlockSpec(memory_space=pltpu.VMEM)
     dma = pltpu.SemaphoreType.DMA((n,))
-    head_rows = 2 * n_state + SUB
+    head_rows = 2 * n_state + 1
     slots = lambda count: [pltpu.VMEM((n, count, width), F32)] * 2
     return pl.pallas_call(
         partial(whole_kernel, n, block),

time: 74.6 us -> 73 us (0.979)
  Pallas kernels: 68.3 us -> 66.8 us
    pallas_call x1, Pallas kernels: 68.3 us -> 66.8 us  [shards(): pl.pallas_call(partial(whole_kernel, n, block), name='whole', in_specs=[v...]
where the time goes in v3:
time: 73 us; the launch traced here: 72.8 us
  Pallas kernels  66.8 us (92%)
  local copies, waits for them, and re-layouts  5.35 us (7%)
    pallas_call x1, Pallas kernels, shards(): pl.pallas_call(partial(whole_kernel, n, block), name='whole', in_specs=[v...  66.8 us
    unnamed x13, local copies, waits for them, and re-layouts  5.35 us

profile of v3, /device:TPU:0, one launch (start us, length us, event | category | flops | bytes accessed | tf_op | source)
XLA Modules:
  0.0 72.8 jit_solution(17867253294952962144)
XLA Ops:
  0.6 66.8 %whole.1 = (bf16[128,4096]{1,0:T(8,128)(2,1)}, bf16[128,4096]{1,0:T(8,128)(2,1)}, f32[16,128]{1,0:T(8,128)}, f32[16,128]{1,0:T(8,128)}, f32[16,128]{1,0:T(8,128)}) custom-call(bf16[128,4096]{1,0:T(8,128)(2,1)} %x_ref.1, bf16[128,4096]{1,0:T(8,128)(2,1)} %d_ref.1, bf16[128,4096]{1,0:T(8,128)(2,1)} %g_ref.1, f32[16,128]{1,0:T(8,128)} %b_ref.1, ...), custom_call_target="tpu_custom_call" | custom-call | tf_op jit(solution)/shard_map/whole/pallas_call | solution.py:267
  67.4 0.0 copy-start
  67.4 2.4 %copy.16 = bf16[128,4096]{1,0:T(8,128)(2,1)} copy(bf16[128,4096]{1,0:T(8,128)(2,1)} %get-tuple-element.10) | data formatting | bytes 2097152
  69.8 0.0 copy-done
  69.8 0.0 copy-start.3
  69.8 1.0 %copy.17 = bf16[128,4096]{1,0:T(8,128)(2,1)} copy(bf16[128,4096]{1,0:T(8,128)(2,1)S(1)} %copy-done) | data formatting | bytes 2097152
  70.8 0.0 copy-done.3
  70.8 0.0 copy-start.2
  70.8 0.6 copy.18
  71.4 0.1 copy-done.2
  71.5 0.0 copy-start.1
  71.5 0.6 copy.19
  72.1 0.1 copy-done.1
  72.2 0.6 copy.20
Async XLA Ops:
  67.4 2.4 %copy-start = (bf16[128,4096]{1,0:T(8,128)(2,1)S(1)}, bf16[128,4096]{1,0:T(8,128)(2,1)}, u32[]{:S(2)}) copy-start(bf16[128,4096]{1,0:T(8,128)(2,1)} %get-tuple-element.11) | copy-start | bytes 3145732
  69.8 1.0 %copy-start.3 = (f32[16,128]{1,0:T(8,128)S(1)}, f32[16,128]{1,0:T(8,128)}, u32[]{:S(2)}) copy-start(f32[16,128]{1,0:T(8,128)} %get-tuple-element.12) | copy-start | bytes 24580
  70.8 0.7 copy-start.2
  71.5 0.7 copy-start.1
